TPU v7x, 32 devices: a whole 2x2x4 slice. The times are simulated.
32 devices in a mesh: basin: 2 (over x), recv: 8 (over z, y), src: 2 (over core).
Axes of the slice: x: 2, y: 2, z: 4, core: 2. Of those that a mesh axis runs over, the one named last changes fastest.
Arguments:
- positions: float32 [3, 4096], P(None, ('basin', 'recv', 'src')), parts along dimension 1, may hold values from -1.1 to 1.1, as said below
- normals: float32 [3, 4096], P(None, ('basin', 'recv', 'src')), parts along dimension 1, may hold values from -1 to 1, as said below
- area: float32 [4096], P(('basin', 'recv', 'src')), parts along dimension 0, may hold values from 0.0009765625 to 0.0078125
- albedo: float32 [4096], P(('basin', 'recv', 'src')), parts along dimension 0, may hold values from 0.1 to 0.6
- conductivity: float32 [4096], P(('basin', 'recv', 'src')), parts along dimension 0, may hold values from 0.05 to 0.4
- soil: float32 [32, 4096], P(None, ('basin', 'recv', 'src')), parts along dimension 1, may hold values from 0.5 to 1.2
- sun_tan: float32 [16], replicated, may hold values from 0.05 to 2
- samples: int32 [32, 32], P(('basin', 'recv', 'src')), parts along dimension 0, may hold values from 1 to 2047
- occupancy: int32 [32, 16], P('basin'), parts along dimension 0, may hold values 0 or 1
Outputs:
- soil_final: float32 [32, 4096], P(None, ('basin', 'recv', 'src')), parts along dimension 1
- bounce: float32 [16, 4096], P(None, ('basin', 'recv', 'src')), parts along dimension 1
There are 2 independent parts, one for each index of `basin`. A program takes and returns all parts, laid end to end along the dimension named above; an argument that names none is the same for every part. Nothing has to cross between parts.
Inputs may be any that keep to these rules, and one draw needn't show every extreme that they name: `positions`: facets lie on a bowl below z = 0. `normals`: each column has unit length.
All inputs are finite; a program needn't handle non-finite values.
Results may differ from a plain program's by a relative error of at most 0.0003.
Values may be sent and summed in bfloat16 or wider, within the bound.
A program may use at most 64 MiB of HBM per device.

v0:
```python
import math
import jax
import jax.numpy as jnp
from jax import lax
from jax.sharding import PartitionSpec as P

solar_flux = 2.0
emissivity = 0.9
surface_gain = 0.1
shade_width = 0.1
reach_offset = 0.05


def partner(value, axis, apart):
    mask = 2**apart
    pairs = [(source, source ^ mask) for source in range(lax.axis_size(axis))]
    return lax.ppermute(value, axis, pairs)


def fourth(value):
    square = value * value
    return square * square


def rotate(values, shift):
    count = values.shape[0]
    doubled = jnp.concatenate([values, values], 0)
    return lax.dynamic_slice_in_dim(doubled, shift, count, 0)


def profile_max(coords, offsets):
    px, py, pz = (coords[0], coords[1], coords[2])
    count = px.shape[0]

    def sweep(best, shift):
        delta_x = rotate(px, shift) - px
        delta_y = rotate(py, shift) - py
        reach = jnp.sqrt(delta_x * delta_x + delta_y * delta_y) + reach_offset
        slope = (rotate(pz, shift) - pz) / reach
        return (jnp.maximum(best, slope), None)

    start = jnp.full((count,), -1e30, jnp.float32)
    best, unused = lax.scan(sweep, start, offsets)
    return best


def horizons(coords, samples):
    return lax.map(lambda offsets: profile_max(coords, offsets), samples)


def sunlight(facing, sun_tan, horizon):
    count = sun_tan.shape[0]
    angle = 2.0 * math.pi * jnp.arange(count, dtype=jnp.float32) / count
    elevation = jnp.arctan(sun_tan)
    sun_x = jnp.cos(elevation) * jnp.cos(angle)
    sun_y = jnp.cos(elevation) * jnp.sin(angle)
    sun_z = jnp.sin(elevation)
    incidence = (
        sun_x[:, None] * facing[0][None, :]
        + sun_y[:, None] * facing[1][None, :]
        + sun_z[:, None] * facing[2][None, :]
    )
    shade = jax.nn.sigmoid((sun_tan[:, None] - horizon) / shade_width)
    return solar_flux * jnp.maximum(incidence, 0.0) * shade


def conduct(soil, direct, bounce, albedo, conductivity):

    def advance(temps, inputs):
        light, scattered = inputs
        grad = temps[1:] - temps[:-1]
        edge = jnp.zeros((1, temps.shape[1]), jnp.float32)
        change = jnp.concatenate([grad, edge], 0) - jnp.concatenate([edge, grad], 0)
        temps = temps + conductivity[None, :] * change
        absorbed = (1.0 - albedo) * (light + scattered)
        top = temps[0] + surface_gain * (absorbed - emissivity * fourth(temps[0]))
        return (jnp.concatenate([top[None, :], temps[1:]], 0), None)

    final, unused = lax.scan(advance, soil, (direct, bounce))
    return final


def view_tile(src_pos, src_nrm, src_area, src_ids, rec_pos, rec_nrm, mask_rows, width):
    onehot = (src_ids[:, None] == jnp.arange(mask_rows.shape[1], dtype=jnp.int32)[None, :]).astype(
        jnp.float32
    )
    weight = jnp.dot(
        onehot, mask_rows.T, preferred_element_type=jnp.float32, precision=lax.Precision.HIGHEST
    )
    weight = jnp.repeat(weight, width, axis=1)
    delta_x = src_pos[0][:, None] - rec_pos[0][None, :]
    delta_y = src_pos[1][:, None] - rec_pos[1][None, :]
    delta_z = src_pos[2][:, None] - rec_pos[2][None, :]
    facing = jnp.maximum(
        rec_nrm[0][None, :] * delta_x
        + rec_nrm[1][None, :] * delta_y
        + rec_nrm[2][None, :] * delta_z,
        0.0,
    )
    toward = jnp.maximum(
        -(
            src_nrm[0][:, None] * delta_x
            + src_nrm[1][:, None] * delta_y
            + src_nrm[2][:, None] * delta_z
        ),
        0.0,
    )
    spread = delta_x * delta_x + delta_y * delta_y + delta_z * delta_z + src_area[:, None]
    return (facing * toward * src_area[:, None] * weight / (math.pi * spread * spread)).astype(
        jnp.bfloat16
    )


def make_fold(src_pos, src_nrm, src_area, block_of, rec_pos, rec_nrm, mask_rows, width):

    def add_tile(carry, segment, begin, count):
        ids = block_of(begin + jnp.arange(count, dtype=jnp.int32))
        pos = lax.dynamic_slice_in_dim(src_pos, begin, count, 1)
        nrm = lax.dynamic_slice_in_dim(src_nrm, begin, count, 1)
        sizes = lax.dynamic_slice_in_dim(src_area, begin, count, 0)
        view = view_tile(pos, nrm, sizes, ids, rec_pos, rec_nrm, mask_rows, width)
        return carry + jnp.dot(segment, view, preferred_element_type=jnp.float32)

    def fold(carry, piece, start):
        count = piece.shape[1]

        def step_once(total, number):
            offset = number * width
            segment = lax.dynamic_slice_in_dim(piece, offset, width, 1)
            return (add_tile(total, segment, offset, width), None)

        total, unused = lax.scan(step_once, carry, jnp.arange(count // width, dtype=jnp.int32))
        return total

    return fold


def body(positions, normals, area, albedo, conductivity, soil, sun_tan, samples, occupancy):
    width = positions.shape[1]
    n_recv = lax.axis_size("recv")
    n_src = lax.axis_size("src")
    recv_index = lax.axis_index("recv")
    src_index = lax.axis_index("src")
    all_pos, all_nrm, all_area = (
        lax.all_gather(positions, ("recv", "src"), axis=1, tiled=True),
        lax.all_gather(normals, ("recv", "src"), axis=1, tiled=True),
        lax.all_gather(area, ("recv", "src"), axis=0, tiled=True),
    )
    horizon = horizons(all_pos, samples)
    facet_horizon = lax.all_to_all(
        horizon.astype(jnp.bfloat16), ("recv", "src"), split_axis=1, concat_axis=0, tiled=True
    ).astype(horizon.dtype)
    direct = sunlight(normals, sun_tan, facet_horizon)
    radiance = (albedo[None, :] * direct + emissivity * fourth(soil[0])[None, :]).astype(
        jnp.bfloat16
    )
    epochs = radiance.shape[0]
    table = occupancy.astype(jnp.float32)
    low_bits = recv_index % 4
    high_bits = recv_index // 4
    share = 4 * n_src
    rec_pos = lax.dynamic_slice_in_dim(all_pos, high_bits * share * width, share * width, 1)
    rec_nrm = lax.dynamic_slice_in_dim(all_nrm, high_bits * share * width, share * width, 1)
    mask_rows = lax.dynamic_slice_in_dim(table, high_bits * share, share, 0)
    column = low_bits * n_src + src_index

    def pick_class(values):
        lead = values.shape[:-1]
        arranged = values.reshape(lead + (n_recv // 4, share * width))
        chosen = lax.dynamic_slice_in_dim(arranged, column * width, width, len(lead) + 1)
        return chosen.reshape(lead + (n_recv // 4 * width,))

    def block_class(index):
        return index // width * share + column

    fold = make_fold(
        pick_class(all_pos),
        pick_class(all_nrm),
        pick_class(all_area),
        block_class,
        rec_pos,
        rec_nrm,
        mask_rows,
        width,
    )
    gathered = radiance
    for bit in range(2, n_recv.bit_length() - 1):
        other = partner(gathered, "recv", bit)
        upper = recv_index // (1 << bit) % 2 == 1
        gathered = jnp.where(
            upper, jnp.concatenate([other, gathered], 1), jnp.concatenate([gathered, other], 1)
        )
    start_sum = jnp.zeros((epochs, share * width), jnp.float32)
    partial_flux = fold(start_sum, gathered, jnp.int32(0))
    paired = lax.psum_scatter(
        partial_flux.reshape(epochs, 4, n_src, width), "src", scatter_dimension=2, tiled=True
    )
    paired = paired.reshape(epochs, 4, width)
    for bit in (1, 0):
        half = paired.shape[1] // 2
        lower = paired[:, :half]
        higher = paired[:, half:]
        upper = recv_index // (1 << bit) % 2 == 1
        keep = jnp.where(upper, higher, lower)
        outgoing = jnp.where(upper, lower, higher)
        paired = keep + partner(outgoing, "recv", bit)
    bounce = paired.reshape(epochs, width)
    final = conduct(soil, direct, bounce, albedo, conductivity)
    return (final, bounce)


def solution(mesh):
    in_specs = (
        P(None, ("basin", "recv", "src")),
        P(None, ("basin", "recv", "src")),
        P(("basin", "recv", "src")),
        P(("basin", "recv", "src")),
        P(("basin", "recv", "src")),
        P(None, ("basin", "recv", "src")),
        P(),
        P(("basin", "recv", "src"), None),
        P("basin", None),
    )
    out_specs = (P(None, ("basin", "recv", "src")), P(None, ("basin", "recv", "src")))
    return jax.shard_map(body, mesh=mesh, in_specs=in_specs, out_specs=out_specs, check_vma=False)
```

profile of v0, /device:TPU:0, one launch (start us, length us, event | category | flops | bytes accessed | tf_op | source)
XLA Modules:
  0.0 205.7 jit_solution(17961653555139462512)
XLA Ops:
  7.2 0.7 copy.50
  7.9 0.7 copy-done.6
  8.6 23.2 %all_gather.9 = f32[3,2048]{1,0:T(4,128)S(1)} all-gather(f32[3,128]{1,0:T(4,128)S(1)} %copy-done.6), channel_id=1, replica_groups=mesh['basin'=2,'recv'=8,'src'=2] {'recv','src'}, dimensions={1}, use_global_device_ids=true | all-gather | bytes 26112 | tf_op jit(solution)/shard_map/all_gather | solution.py:145
  32.5 91.5 %while.43 = (s32[]{:T(128)}, bf16[2048]{0:T(1024)(128)(2,1)S(1)}, s32[32]{0:T(128)S(1)}, f32[4096]{0:T(1024)S(1)}, f32[2048]{0:T(1024)S(1)}, /*index=5*/f32[4096...) while((s32[]{:T(128)}, bf16[2048]{0:T(1024)(128)(2,1)S(1)}, ...), condition=%wide.region_1.2_spmd.clone, body=%wide.region_0.1_spmd.clone.sunk | while | flops 24582 | bytes 57529 | solution.py:43
  35.3 0.7 dynamic_slice.136
  38.2 0.7 dynamic_slice.136
  41.0 0.7 dynamic_slice.136
  43.9 0.7 dynamic_slice.136
  46.7 0.7 dynamic_slice.136
  49.6 0.7 dynamic_slice.136
  52.5 0.7 dynamic_slice.136
  55.3 0.7 dynamic_slice.136
  58.2 0.7 dynamic_slice.136
  61.0 0.7 dynamic_slice.136
  78.2 0.7 dynamic_slice.136
  81.0 0.7 dynamic_slice.136
  83.9 0.7 dynamic_slice.136
  86.8 0.7 dynamic_slice.136
  124.5 3.5 %all-to-all-start = ((bf16[1,16,128]{2,0,1:T(2,128)(2,1)}), bf16[1,16,128]{2,0,1:T(2,128)(2,1)S(1)}, u32[]{:S(2)}, u32[]{:S(2)}) async-start(bf16[1,16,128]{2,0,1:T(2,128)(2,1)} %copy.16), calls=%async_computation | async-start | bytes 16384 | tf_op jit(solution)/shard_map/all_to_all | solution.py:150
  128.7 21.7 %all_gather.10 = f32[3,2048]{1,0:T(4,128)S(1)} all-gather(f32[3,128]{1,0:T(4,128)S(1)} %copy-done.5), channel_id=1, replica_groups=mesh['basin'=2,'recv'=8,'src'=2] {'recv','src'}, dimensions={1}, use_global_device_ids=true | all-gather | bytes 26112 | tf_op jit(solution)/shard_map/all_gather | solution.py:146
  152.0 17.4 %all-gather = f32[16,1,128]{2,1,0:T(1,128)S(1)} all-gather(f32[1,1,128]{2,1,0:T(1,128)S(1)} %bitcast.108), channel_id=1, replica_groups=mesh['basin'=2,'recv'=8,'src'=2] {'recv','src'}, dimensions={0}, use_global_device_ids=true | all-gather | bytes 8704 | tf_op jit(solution)/shard_map/all_gather | solution.py:147
  171.5 4.4 %collective-permute-done = bf16[16,128]{1,0:T(8,128)(2,1)S(1)} collective-permute-done((bf16[16,128]{1,0:T(8,128)(2,1)S(1)}, bf16[16,128]{1,0:T(8,128)(2,1)S(1)}, u32[]{:S(2)}, u32[]{:S(2)}) %collective-permute-start) | collective-permute-done | bytes 4128 | tf_op jit(solution)/shard_map/ppermute | solution.py:17
  175.9 5.1 %while.44 = (s32[]{:T(128)}, f32[16,1024]{1,0:T(8,128)S(1)}, s32[2]{0:T(128)S(1)}, bf16[16,256]{1,0:T(8,128)(2,1)S(1)}, f32[3,1024]{1,0:T(4,128)S(1)}, /*index=5...) while((s32[]{:T(128)}, f32[16,1024]{1,0:T(8,128)S(1)}, ...), condition=%wide.region_3.4_spmd.clone, body=%wide.region_2.3_spmd.clone.sunk | while | flops 8229127 | bytes 1284333 | solution.py:132
  177.6 0.8 convolution_add_fusion.2
  180.2 0.8 convolution_add_fusion.2
  181.7 6.1 %reduce-scatter.2.cloned.1.call-done = f32[16,4,1,128]{3,0,1,2:T(8,128)} async-done(((f32[16,4,2,128]{3,0,1,2:T(8,128)}), f32[16,4,1,128]{3,0,1,2:T(8,128)}) %reduce-scatter.2.cloned.1.call-update) | async-done | bytes 32784 | tf_op jit(solution)/shard_map/reduce_scatter | solution.py:195
  187.8 0.8 slice_select_fusion
  188.6 1.7 collective-permute-start.1
  190.3 2.1 %collective-permute-done.1 = f32[16,2,128]{2,0,1:T(8,128)S(1)} collective-permute-done((f32[16,2,128]{2,0,1:T(8,128)S(1)}, f32[16,2,128]{2,0,1:T(8,128)S(1)}, u32[]{:S(2)}, u32[]{:S(2)}) %collective-permute-start.1) | collective-permute-done | bytes 16416 | tf_op jit(solution)/shard_map/ppermute | solution.py:17
  192.4 1.7 collective-permute-start.2
  194.1 2.0 collective-permute-done.2
  196.7 1.5 while.42
  (204 shorter events, 25.5 us)
Async XLA Ops:
  7.9 0.7 copy-start.6
  31.8 0.7 copy-start.10
  124.5 46.0 %all-to-all-start = ((bf16[1,16,128]{2,0,1:T(2,128)(2,1)}), bf16[1,16,128]{2,0,1:T(2,128)(2,1)S(1)}, u32[]{:S(2)}, u32[]{:S(2)}) async-start(bf16[1,16,128]{2,0,1:T(2,128)(2,1)} %copy.16), calls=%async_computation | async-start | bytes 16384 | tf_op jit(solution)/shard_map/all_to_all | solution.py:150
  128.0 59.8 %reduce-scatter.2.cloned.1.call-start = ((), (), s32[]{:S(2)}) async-start(), calls=%async_computation.2 | async-start | bytes 98304 | tf_op jit(solution)/shard_map/reduce_scatter | solution.py:195
  128.1 0.7 copy-start.5
  150.5 0.7 copy-start.8
  150.5 0.7 copy-start.7
  151.3 0.7 copy-start.9
  170.6 0.7 copy-start.2
  171.3 4.6 %collective-permute-start = (bf16[16,128]{1,0:T(8,128)(2,1)S(1)}, bf16[16,128]{1,0:T(8,128)(2,1)S(1)}, u32[]{:S(2)}, u32[]{:S(2)}) collective-permute-start(bf16[16,128]{1,0:T(8,128)(2,1)S(1)} %get-tuple-element.374), channel_id=1, source_target_pairs={{0,8},{2,10},{4,12},{6,14},{8,0},{10,2},{12,4},{14,6},{1,9},{3,11}... | collective-permute-start | bytes 12296 | tf_op jit(solution)/shard_map/ppermute | solution.py:17
  187.8 4.5 %copy-start.1 = (f32[16,4,1,128]{3,0,1,2:T(8,128)S(1)}, f32[16,4,1,128]{3,0,1,2:T(8,128)}, u32[]{:S(2)}) copy-start(f32[16,4,1,128]{3,0,1,2:T(8,128)} %reduce-scatter.2.cloned.1.call-done) | copy-start | bytes 98308
  188.6 3.7 %collective-permute-start.1 = (f32[16,2,128]{2,0,1:T(8,128)S(1)}, f32[16,2,128]{2,0,1:T(8,128)S(1)}, u32[]{:S(2)}, u32[]{:S(2)}) collective-permute-start(f32[16,2,128]{2,0,1:T(8,128)S(1)} %slice_select_fusion), channel_id=1, source_target_pairs={{0,4},{2,6},{4,0},{6,2},{8,12},{10,14},{12,8},{14,10},{1,5},{3,7},... | collective-permute-start | bytes 49160 | tf_op jit(solution)/shard_map/ppermute | solution.py:17
  192.4 3.7 %collective-permute-start.2 = (f32[16,1,128]{2,0,1:T(8,128)S(1)}, f32[16,1,128]{2,0,1:T(8,128)S(1)}, u32[]{:S(2)}, u32[]{:S(2)}) collective-permute-start(f32[16,1,128]{2,0,1:T(8,128)S(1)} %slice_select_fusion.1), channel_id=1, source_target_pairs={{0,2},{2,0},{4,6},{6,4},{8,10},{10,8},{12,14},{14,12},{1,3},{3,1},... | collective-permute-start | bytes 24584 | tf_op jit(solution)/shard_map/ppermute | solution.py:17
  196.1 0.7 copy-start.4
  198.3 0.6 copy-start
  198.3 0.6 copy-start.3
Sparse Core Ops, SparseCore 0:
  181.8 5.9 reduce-scatter.1
where the time goes:
time: 207 us; the launch traced here: 206 us
  loops' own time  68.9 us (33%)
  blocking collectives  62.3 us (30%)
  local copies, waits for them, and re-layouts  31 us (15%)
  waiting for transfers between devices  14.5 us (7%)
  between operations  14.4 us (7%)
  starting transfers between devices  7 us (3%)
  other arithmetic  5.43 us (3%)
    another operation x1, loops' own time, profile_max(): best, unused = lax.scan(sweep, start, offsets)  67 us
    all_gather x1, blocking collectives, body(): lax.all_gather(positions, ('recv', 'src'), axis=1, tiled=True)  23.2 us
    all_gather x1, blocking collectives, body(): lax.all_gather(normals, ('recv', 'src'), axis=1, tiled=True)  21.7 us
    dynamic_slice x32, local copies, waits for them, and re-layouts, profile_max(): best, unused = lax.scan(sweep, start, offsets)  21.4 us
    all_gather x1, blocking collectives, body(): lax.all_gather(area, ('recv', 'src'), axis=0, tiled=True)  17.4 us
    ppermute x3, waiting for transfers between devices, partner(): return lax.ppermute(value, axis, pairs)  8.45 us
    reduce_scatter x1, waiting for transfers between devices, body(): lax.psum_scatter(partial_flux.reshape(epochs, 4, n_src, width), 'src', sc...  6.07 us
    unnamed x27, local copies, waits for them, and re-layouts  5.88 us
  transfers between devices with their start and end apart: 5, of which 4 were waited for; matrix products, arithmetic and copies ran while one was open for 1% of the time, Pallas kernels for 0%

commit v1 on v0

--- a/solution.py
+++ b/solution.py
@@ -9,6 +9,19 @@
 surface_gain = 0.1
 shade_width = 0.1
 reach_offset = 0.05
+
+
+def ring_gather(value, axis, dim):
+    size, position, extent = (lax.axis_size(axis), lax.axis_index(axis), value.shape[dim])
+    right = [(i, (i + 1) % size) for i in range(size)]
+    out = jnp.zeros((*value.shape[:dim], size * extent, *value.shape[dim + 1 :]), value.dtype)
+    held = value
+    for turn in range(size):
+        owner = (position - turn) % size
+        out = lax.dynamic_update_slice_in_dim(out, held, owner * extent, axis=dim)
+        if turn < size - 1:
+            held = lax.ppermute(held, axis, right)
+    return out
 
 
 def partner(value, axis, apart):
@@ -142,7 +155,7 @@
     recv_index = lax.axis_index("recv")
     src_index = lax.axis_index("src")
     all_pos, all_nrm, all_area = (
-        lax.all_gather(positions, ("recv", "src"), axis=1, tiled=True),
+        ring_gather(positions, ("recv", "src"), 1),
         lax.all_gather(normals, ("recv", "src"), axis=1, tiled=True),
         lax.all_gather(area, ("recv", "src"), axis=0, tiled=True),
     )

time: 207 us -> 257 us (1.24)
  waiting for transfers between devices: 14.5 us -> 98.6 us
  blocking collectives: 62.3 us -> 40.1 us
  loops' own time: 68.9 us -> 58.2 us
    ppermute x0 -> x15, waiting for transfers between devices: none -> 79.4 us  [ring_gather(): held = lax.ppermute(held, axis, right)]
    all_gather x1 -> x0, blocking collectives: 23.2 us -> none  [body(): lax.all_gather(positions, ('recv', 'src'), axis=1, tiled=True)]
    another operation x1, loops' own time: 67 us -> 56.1 us  [profile_max(): best, unused = lax.scan(sweep, start, offsets)]
    all_to_all x1, waiting for transfers between devices: 0.01 us -> 6.22 us  [body(): lax.all_to_all(horizon.astype(jnp.bfloat16), ('recv', 'src'), split_axis=...]
  transfers between devices with their start and end apart: 5 -> 20, of which waited for: 4 -> 19; matrix products, arithmetic and copies ran while one was open for 1% -> 1% of each run, Pallas kernels for 0% -> 0%
where the time goes in v1:
time: 257 us; the launch traced here: 256 us
  waiting for transfers between devices  98.6 us (38%)
  loops' own time  58.2 us (23%)
  blocking collectives  40.1 us (16%)
  local copies, waits for them, and re-layouts  28.9 us (11%)
  between operations  14.4 us (6%)
  starting transfers between devices  8.46 us (3%)
  other arithmetic  5.45 us (2%)
    ppermute x15, waiting for transfers between devices, ring_gather(): held = lax.ppermute(held, axis, right)  79.4 us
    another operation x1, loops' own time, profile_max(): best, unused = lax.scan(sweep, start, offsets)  56.1 us
    all_gather x1, blocking collectives, body(): lax.all_gather(normals, ('recv', 'src'), axis=1, tiled=True)  22.7 us
    dynamic_slice x32, local copies, waits for them, and re-layouts, profile_max(): best, unused = lax.scan(sweep, start, offsets)  19 us
    all_gather x1, blocking collectives, body(): lax.all_gather(area, ('recv', 'src'), axis=0, tiled=True)  17.4 us
    ppermute x3, waiting for transfers between devices, partner(): return lax.ppermute(value, axis, pairs)  7.99 us
    all_to_all x1, waiting for transfers between devices, body(): lax.all_to_all(horizon.astype(jnp.bfloat16), ('recv', 'src'), split_axis=...  6.22 us
    unnamed x27, local copies, waits for them, and re-layouts  5.93 us
  transfers between devices with their start and end apart: 20, of which 19 were waited for; matrix products, arithmetic and copies ran while one was open for 1% of the time, Pallas kernels for 0%

profile of v1, /device:TPU:0, one launch (start us, length us, event | category | flops | bytes accessed | tf_op | source)
XLA Modules:
  0.0 256.1 jit_solution(10878962373876687224)
XLA Ops:
  7.2 0.7 copy.66
  8.4 0.7 copy-done.5
  9.1 22.7 %all_gather.6 = f32[3,2048]{1,0:T(4,128)S(1)} all-gather(f32[3,128]{1,0:T(4,128)S(1)} %copy-done.5), channel_id=1, replica_groups=mesh['basin'=2,'recv'=8,'src'=2] {'recv','src'}, dimensions={1}, use_global_device_ids=true | all-gather | bytes 26112 | tf_op jit(solution)/shard_map/all_gather | solution.py:159
  33.2 17.4 %all-gather = f32[16,1,128]{2,1,0:T(1,128)S(1)} all-gather(f32[1,1,128]{2,1,0:T(1,128)S(1)} %bitcast.108), channel_id=1, replica_groups=mesh['basin'=2,'recv'=8,'src'=2] {'recv','src'}, dimensions={0}, use_global_device_ids=true | all-gather | bytes 8704 | tf_op jit(solution)/shard_map/all_gather | solution.py:160
  53.1 5.4 %collective-permute-done.1 = f32[3,128]{1,0:T(4,128)S(1)} collective-permute-done((f32[3,128]{1,0:T(4,128)S(1)}, f32[3,128]{1,0:T(4,128)S(1)}, u32[]{:S(2)}, u32[]{:S(2)}) %collective-permute-start.1) | collective-permute-done | bytes 1568 | tf_op jit(solution)/shard_map/ppermute | solution.py:23
  58.5 5.7 %collective-permute-done.2 = f32[3,128]{1,0:T(4,128)S(1)} collective-permute-done((f32[3,128]{1,0:T(4,128)S(1)}, f32[3,128]{1,0:T(4,128)S(1)}, u32[]{:S(2)}, u32[]{:S(2)}) %collective-permute-start.2) | collective-permute-done | bytes 1568 | tf_op jit(solution)/shard_map/ppermute | solution.py:23
  64.2 5.7 %collective-permute-done.3 = f32[3,128]{1,0:T(4,128)S(1)} collective-permute-done((f32[3,128]{1,0:T(4,128)S(1)}, f32[3,128]{1,0:T(4,128)S(1)}, u32[]{:S(2)}, u32[]{:S(2)}) %collective-permute-start.3) | collective-permute-done | bytes 1568 | tf_op jit(solution)/shard_map/ppermute | solution.py:23
  69.9 5.7 %collective-permute-done.4 = f32[3,128]{1,0:T(4,128)S(1)} collective-permute-done((f32[3,128]{1,0:T(4,128)S(1)}, f32[3,128]{1,0:T(4,128)S(1)}, u32[]{:S(2)}, u32[]{:S(2)}) %collective-permute-start.4) | collective-permute-done | bytes 1568 | tf_op jit(solution)/shard_map/ppermute | solution.py:23
  75.6 5.7 %collective-permute-done.5 = f32[3,128]{1,0:T(4,128)S(1)} collective-permute-done((f32[3,128]{1,0:T(4,128)S(1)}, f32[3,128]{1,0:T(4,128)S(1)}, u32[]{:S(2)}, u32[]{:S(2)}) %collective-permute-start.5) | collective-permute-done | bytes 1568 | tf_op jit(solution)/shard_map/ppermute | solution.py:23
  81.3 5.7 %collective-permute-done.6 = f32[3,128]{1,0:T(4,128)S(1)} collective-permute-done((f32[3,128]{1,0:T(4,128)S(1)}, f32[3,128]{1,0:T(4,128)S(1)}, u32[]{:S(2)}, u32[]{:S(2)}) %collective-permute-start.6) | collective-permute-done | bytes 1568 | tf_op jit(solution)/shard_map/ppermute | solution.py:23
  87.0 5.7 %collective-permute-done.7 = f32[3,128]{1,0:T(4,128)S(1)} collective-permute-done((f32[3,128]{1,0:T(4,128)S(1)}, f32[3,128]{1,0:T(4,128)S(1)}, u32[]{:S(2)}, u32[]{:S(2)}) %collective-permute-start.7) | collective-permute-done | bytes 1568 | tf_op jit(solution)/shard_map/ppermute | solution.py:23
  92.7 5.7 %collective-permute-done.8 = f32[3,128]{1,0:T(4,128)S(1)} collective-permute-done((f32[3,128]{1,0:T(4,128)S(1)}, f32[3,128]{1,0:T(4,128)S(1)}, u32[]{:S(2)}, u32[]{:S(2)}) %collective-permute-start.8) | collective-permute-done | bytes 1568 | tf_op jit(solution)/shard_map/ppermute | solution.py:23
  98.4 5.7 %collective-permute-done.9 = f32[3,128]{1,0:T(4,128)S(1)} collective-permute-done((f32[3,128]{1,0:T(4,128)S(1)}, f32[3,128]{1,0:T(4,128)S(1)}, u32[]{:S(2)}, u32[]{:S(2)}) %collective-permute-start.9) | collective-permute-done | bytes 1568 | tf_op jit(solution)/shard_map/ppermute | solution.py:23
  104.1 5.7 %collective-permute-done.10 = f32[3,128]{1,0:T(4,128)S(1)} collective-permute-done((f32[3,128]{1,0:T(4,128)S(1)}, f32[3,128]{1,0:T(4,128)S(1)}, u32[]{:S(2)}, u32[]{:S(2)}) %collective-permute-start.10) | collective-permute-done | bytes 1568 | tf_op jit(solution)/shard_map/ppermute | solution.py:23
  109.8 5.7 %collective-permute-done.11 = f32[3,128]{1,0:T(4,128)S(1)} collective-permute-done((f32[3,128]{1,0:T(4,128)S(1)}, f32[3,128]{1,0:T(4,128)S(1)}, u32[]{:S(2)}, u32[]{:S(2)}) %collective-permute-start.11) | collective-permute-done | bytes 1568 | tf_op jit(solution)/shard_map/ppermute | solution.py:23
  115.5 5.7 %collective-permute-done.12 = f32[3,128]{1,0:T(4,128)S(1)} collective-permute-done((f32[3,128]{1,0:T(4,128)S(1)}, f32[3,128]{1,0:T(4,128)S(1)}, u32[]{:S(2)}, u32[]{:S(2)}) %collective-permute-start.12) | collective-permute-done | bytes 1568 | tf_op jit(solution)/shard_map/ppermute | solution.py:23
  121.2 5.7 %collective-permute-done.13 = f32[3,128]{1,0:T(4,128)S(1)} collective-permute-done((f32[3,128]{1,0:T(4,128)S(1)}, f32[3,128]{1,0:T(4,128)S(1)}, u32[]{:S(2)}, u32[]{:S(2)}) %collective-permute-start.13) | collective-permute-done | bytes 1568 | tf_op jit(solution)/shard_map/ppermute | solution.py:23
  127.0 5.7 %collective-permute-done.14 = f32[3,128]{1,0:T(4,128)S(1)} collective-permute-done((f32[3,128]{1,0:T(4,128)S(1)}, f32[3,128]{1,0:T(4,128)S(1)}, u32[]{:S(2)}, u32[]{:S(2)}) %collective-permute-start.14) | collective-permute-done | bytes 1568 | tf_op jit(solution)/shard_map/ppermute | solution.py:23
  133.4 78.2 %while.43 = (s32[]{:T(128)}, bf16[2048]{0:T(1024)(128)(2,1)S(1)}, s32[32]{0:T(128)S(1)}, f32[4096]{0:T(1024)S(1)}, f32[2048]{0:T(1024)S(1)}, /*index=5*/f32[4096...) while((s32[]{:T(128)}, bf16[2048]{0:T(1024)(128)(2,1)S(1)}, ...), condition=%wide.region_1.2_spmd.clone, body=%wide.region_0.1_spmd.clone.sunk | while | flops 24582 | bytes 57529 | solution.py:56
  212.2 3.5 %all-to-all-start = ((bf16[1,16,128]{2,0,1:T(2,128)(2,1)}), bf16[1,16,128]{2,0,1:T(2,128)(2,1)S(1)}, u32[]{:S(2)}, u32[]{:S(2)}) async-start(bf16[1,16,128]{2,0,1:T(2,128)(2,1)} %copy.16), calls=%async_computation | async-start | bytes 16384 | tf_op jit(solution)/shard_map/all_to_all | solution.py:163
  215.8 6.2 %all-to-all-done = bf16[1,16,128]{2,0,1:T(2,128)(2,1)S(1)} async-done(((bf16[1,16,128]{2,0,1:T(2,128)(2,1)}), bf16[1,16,128]{2,0,1:T(2,128)(2,1)S(1)}, u32[]{:S(2)}, u32[]{:S(2)}) %all-to-all-start) | async-done | bytes 4128 | tf_op jit(solution)/shard_map/all_to_all | solution.py:163
  223.3 4.0 %collective-permute-done.15 = bf16[16,128]{1,0:T(8,128)(2,1)S(1)} collective-permute-done((bf16[16,128]{1,0:T(8,128)(2,1)S(1)}, bf16[16,128]{1,0:T(8,128)(2,1)S(1)}, u32[]{:S(2)}, u32[]{:S(2)}) %collective-permute-start.15) | collective-permute-done | bytes 4128 | tf_op jit(solution)/shard_map/ppermute | solution.py:30
  227.3 5.2 %while.44 = (s32[]{:T(128)}, f32[16,1024]{1,0:T(8,128)S(1)}, s32[2]{0:T(128)S(1)}, bf16[16,256]{1,0:T(8,128)(2,1)S(1)}, f32[3,1024]{1,0:T(4,128)S(1)}, /*index=5...) while((s32[]{:T(128)}, f32[16,1024]{1,0:T(8,128)S(1)}, ...), condition=%wide.region_3.4_spmd.clone, body=%wide.region_2.3_spmd.clone.sunk | while | flops 8229127 | bytes 1284333 | solution.py:145
  229.1 0.8 convolution_add_fusion.2
  231.7 0.8 convolution_add_fusion.2
  233.3 4.9 %reduce-scatter.2.cloned.1.call-done = f32[16,4,1,128]{3,0,1,2:T(8,128)} async-done(((f32[16,4,2,128]{3,0,1,2:T(8,128)}), f32[16,4,1,128]{3,0,1,2:T(8,128)}) %reduce-scatter.2.cloned.1.call-update) | async-done | bytes 32784 | tf_op jit(solution)/shard_map/reduce_scatter | solution.py:208
  238.2 0.8 slice_select_fusion
  239.0 1.7 collective-permute-start.16
  240.7 2.1 collective-permute-done.16
  242.8 1.8 collective-permute-start.17
  244.5 2.0 collective-permute-done.17
  247.2 1.5 while.42
  (250 shorter events, 34.1 us)
Async XLA Ops:
  7.2 0.7 copy-start.7
  7.9 44.8 %collective-permute-start = (f32[3,128]{1,0:T(4,128)S(1)}, f32[3,128]{1,0:T(4,128)S(1)}, u32[]{:S(2)}, u32[]{:S(2)}) collective-permute-start(f32[3,128]{1,0:T(4,128)S(1)} %copy-done.7), channel_id=1, source_target_pairs={{0,1},{1,2},{2,3},{3,4},{4,5},{5,6},{6,7},{7,8},{8,9},{9,10},{10,1... | collective-permute-start | bytes 4616 | tf_op jit(solution)/shard_map/ppermute | solution.py:23
  8.4 0.7 copy-start.5
  31.8 0.7 copy-start.8
  32.5 0.7 copy-start.9
  51.8 0.7 copy-start.6
  52.7 5.8 %collective-permute-start.1 = (f32[3,128]{1,0:T(4,128)S(1)}, f32[3,128]{1,0:T(4,128)S(1)}, u32[]{:S(2)}, u32[]{:S(2)}) collective-permute-start(f32[3,128]{1,0:T(4,128)S(1)} %collective-permute-done), channel_id=1, source_target_pairs={{0,1},{1,2},{2,3},{3,4},{4,5},{5,6},{6,7},{7,8},{8,9},{9,10},{10,1... | collective-permute-start | bytes 4616 | tf_op jit(solution)/shard_map/ppermute | solution.py:23
  58.4 5.7 %collective-permute-start.2 = (f32[3,128]{1,0:T(4,128)S(1)}, f32[3,128]{1,0:T(4,128)S(1)}, u32[]{:S(2)}, u32[]{:S(2)}) collective-permute-start(f32[3,128]{1,0:T(4,128)S(1)} %collective-permute-done.1), channel_id=1, source_target_pairs={{0,1},{1,2},{2,3},{3,4},{4,5},{5,6},{6,7},{7,8},{8,9},{9,10},{10,1... | collective-permute-start | bytes 4616 | tf_op jit(solution)/shard_map/ppermute | solution.py:23
  64.2 5.7 %collective-permute-start.3 = (f32[3,128]{1,0:T(4,128)S(1)}, f32[3,128]{1,0:T(4,128)S(1)}, u32[]{:S(2)}, u32[]{:S(2)}) collective-permute-start(f32[3,128]{1,0:T(4,128)S(1)} %collective-permute-done.2), channel_id=1, source_target_pairs={{0,1},{1,2},{2,3},{3,4},{4,5},{5,6},{6,7},{7,8},{8,9},{9,10},{10,1... | collective-permute-start | bytes 4616 | tf_op jit(solution)/shard_map/ppermute | solution.py:23
  69.9 5.7 %collective-permute-start.4 = (f32[3,128]{1,0:T(4,128)S(1)}, f32[3,128]{1,0:T(4,128)S(1)}, u32[]{:S(2)}, u32[]{:S(2)}) collective-permute-start(f32[3,128]{1,0:T(4,128)S(1)} %collective-permute-done.3), channel_id=1, source_target_pairs={{0,1},{1,2},{2,3},{3,4},{4,5},{5,6},{6,7},{7,8},{8,9},{9,10},{10,1... | collective-permute-start | bytes 4616 | tf_op jit(solution)/shard_map/ppermute | solution.py:23
  75.6 5.7 %collective-permute-start.5 = (f32[3,128]{1,0:T(4,128)S(1)}, f32[3,128]{1,0:T(4,128)S(1)}, u32[]{:S(2)}, u32[]{:S(2)}) collective-permute-start(f32[3,128]{1,0:T(4,128)S(1)} %collective-permute-done.4), channel_id=1, source_target_pairs={{0,1},{1,2},{2,3},{3,4},{4,5},{5,6},{6,7},{7,8},{8,9},{9,10},{10,1... | collective-permute-start | bytes 4616 | tf_op jit(solution)/shard_map/ppermute | solution.py:23
  81.3 5.7 %collective-permute-start.6 = (f32[3,128]{1,0:T(4,128)S(1)}, f32[3,128]{1,0:T(4,128)S(1)}, u32[]{:S(2)}, u32[]{:S(2)}) collective-permute-start(f32[3,128]{1,0:T(4,128)S(1)} %collective-permute-done.5), channel_id=1, source_target_pairs={{0,1},{1,2},{2,3},{3,4},{4,5},{5,6},{6,7},{7,8},{8,9},{9,10},{10,1... | collective-permute-start | bytes 4616 | tf_op jit(solution)/shard_map/ppermute | solution.py:23
  87.0 5.7 %collective-permute-start.7 = (f32[3,128]{1,0:T(4,128)S(1)}, f32[3,128]{1,0:T(4,128)S(1)}, u32[]{:S(2)}, u32[]{:S(2)}) collective-permute-start(f32[3,128]{1,0:T(4,128)S(1)} %collective-permute-done.6), channel_id=1, source_target_pairs={{0,1},{1,2},{2,3},{3,4},{4,5},{5,6},{6,7},{7,8},{8,9},{9,10},{10,1... | collective-permute-start | bytes 4616 | tf_op jit(solution)/shard_map/ppermute | solution.py:23
  92.7 5.7 %collective-permute-start.8 = (f32[3,128]{1,0:T(4,128)S(1)}, f32[3,128]{1,0:T(4,128)S(1)}, u32[]{:S(2)}, u32[]{:S(2)}) collective-permute-start(f32[3,128]{1,0:T(4,128)S(1)} %collective-permute-done.7), channel_id=1, source_target_pairs={{0,1},{1,2},{2,3},{3,4},{4,5},{5,6},{6,7},{7,8},{8,9},{9,10},{10,1... | collective-permute-start | bytes 4616 | tf_op jit(solution)/shard_map/ppermute | solution.py:23
  98.4 5.7 %collective-permute-start.9 = (f32[3,128]{1,0:T(4,128)S(1)}, f32[3,128]{1,0:T(4,128)S(1)}, u32[]{:S(2)}, u32[]{:S(2)}) collective-permute-start(f32[3,128]{1,0:T(4,128)S(1)} %collective-permute-done.8), channel_id=1, source_target_pairs={{0,1},{1,2},{2,3},{3,4},{4,5},{5,6},{6,7},{7,8},{8,9},{9,10},{10,1... | collective-permute-start | bytes 4616 | tf_op jit(solution)/shard_map/ppermute | solution.py:23
  104.1 5.7 %collective-permute-start.10 = (f32[3,128]{1,0:T(4,128)S(1)}, f32[3,128]{1,0:T(4,128)S(1)}, u32[]{:S(2)}, u32[]{:S(2)}) collective-permute-start(f32[3,128]{1,0:T(4,128)S(1)} %collective-permute-done.9), channel_id=1, source_target_pairs={{0,1},{1,2},{2,3},{3,4},{4,5},{5,6},{6,7},{7,8},{8,9},{9,10},{10,1... | collective-permute-start | bytes 4616 | tf_op jit(solution)/shard_map/ppermute | solution.py:23
  109.8 5.7 %collective-permute-start.11 = (f32[3,128]{1,0:T(4,128)S(1)}, f32[3,128]{1,0:T(4,128)S(1)}, u32[]{:S(2)}, u32[]{:S(2)}) collective-permute-start(f32[3,128]{1,0:T(4,128)S(1)} %collective-permute-done.10), channel_id=1, source_target_pairs={{0,1},{1,2},{2,3},{3,4},{4,5},{5,6},{6,7},{7,8},{8,9},{9,10},{10,1... | collective-permute-start | bytes 4616 | tf_op jit(solution)/shard_map/ppermute | solution.py:23
  115.5 5.7 %collective-permute-start.12 = (f32[3,128]{1,0:T(4,128)S(1)}, f32[3,128]{1,0:T(4,128)S(1)}, u32[]{:S(2)}, u32[]{:S(2)}) collective-permute-start(f32[3,128]{1,0:T(4,128)S(1)} %collective-permute-done.11), channel_id=1, source_target_pairs={{0,1},{1,2},{2,3},{3,4},{4,5},{5,6},{6,7},{7,8},{8,9},{9,10},{10,1... | collective-permute-start | bytes 4616 | tf_op jit(solution)/shard_map/ppermute | solution.py:23
  121.2 5.7 %collective-permute-start.13 = (f32[3,128]{1,0:T(4,128)S(1)}, f32[3,128]{1,0:T(4,128)S(1)}, u32[]{:S(2)}, u32[]{:S(2)}) collective-permute-start(f32[3,128]{1,0:T(4,128)S(1)} %collective-permute-done.12), channel_id=1, source_target_pairs={{0,1},{1,2},{2,3},{3,4},{4,5},{5,6},{6,7},{7,8},{8,9},{9,10},{10,1... | collective-permute-start | bytes 4616 | tf_op jit(solution)/shard_map/ppermute | solution.py:23
  126.9 5.7 %collective-permute-start.14 = (f32[3,128]{1,0:T(4,128)S(1)}, f32[3,128]{1,0:T(4,128)S(1)}, u32[]{:S(2)}, u32[]{:S(2)}) collective-permute-start(f32[3,128]{1,0:T(4,128)S(1)} %collective-permute-done.13), channel_id=1, source_target_pairs={{0,1},{1,2},{2,3},{3,4},{4,5},{5,6},{6,7},{7,8},{8,9},{9,10},{10,1... | collective-permute-start | bytes 4616 | tf_op jit(solution)/shard_map/ppermute | solution.py:23
  132.7 0.7 copy-start.10
  212.2 9.8 %all-to-all-start = ((bf16[1,16,128]{2,0,1:T(2,128)(2,1)}), bf16[1,16,128]{2,0,1:T(2,128)(2,1)S(1)}, u32[]{:S(2)}, u32[]{:S(2)}) async-start(bf16[1,16,128]{2,0,1:T(2,128)(2,1)} %copy.16), calls=%async_computation | async-start | bytes 16384 | tf_op jit(solution)/shard_map/all_to_all | solution.py:163
  215.7 22.6 %reduce-scatter.2.cloned.1.call-start = ((), (), s32[]{:S(2)}) async-start(), calls=%async_computation.2 | async-start | bytes 98304 | tf_op jit(solution)/shard_map/reduce_scatter | solution.py:208
  222.0 0.7 copy-start.2
  222.7 4.6 %collective-permute-start.15 = (bf16[16,128]{1,0:T(8,128)(2,1)S(1)}, bf16[16,128]{1,0:T(8,128)(2,1)S(1)}, u32[]{:S(2)}, u32[]{:S(2)}) collective-permute-start(bf16[16,128]{1,0:T(8,128)(2,1)S(1)} %get-tuple-element.374), channel_id=1, source_target_pairs={{0,8},{2,10},{4,12},{6,14},{8,0},{10,2},{12,4},{14,6},{1,9},{3,11}... | collective-permute-start | bytes 12296 | tf_op jit(solution)/shard_map/ppermute | solution.py:30
  238.2 4.5 %copy-start.1 = (f32[16,4,1,128]{3,0,1,2:T(8,128)S(1)}, f32[16,4,1,128]{3,0,1,2:T(8,128)}, u32[]{:S(2)}) copy-start(f32[16,4,1,128]{3,0,1,2:T(8,128)} %reduce-scatter.2.cloned.1.call-done) | copy-start | bytes 98308
  239.0 3.7 %collective-permute-start.16 = (f32[16,2,128]{2,0,1:T(8,128)S(1)}, f32[16,2,128]{2,0,1:T(8,128)S(1)}, u32[]{:S(2)}, u32[]{:S(2)}) collective-permute-start(f32[16,2,128]{2,0,1:T(8,128)S(1)} %slice_select_fusion), channel_id=1, source_target_pairs={{0,4},{2,6},{4,0},{6,2},{8,12},{10,14},{12,8},{14,10},{1,5},{3,7},... | collective-permute-start | bytes 49160 | tf_op jit(solution)/shard_map/ppermute | solution.py:30
  242.8 3.7 %collective-permute-start.17 = (f32[16,1,128]{2,0,1:T(8,128)S(1)}, f32[16,1,128]{2,0,1:T(8,128)S(1)}, u32[]{:S(2)}, u32[]{:S(2)}) collective-permute-start(f32[16,1,128]{2,0,1:T(8,128)S(1)} %slice_select_fusion.1), channel_id=1, source_target_pairs={{0,2},{2,0},{4,6},{6,4},{8,10},{10,8},{12,14},{14,12},{1,3},{3,1},... | collective-permute-start | bytes 24584 | tf_op jit(solution)/shard_map/ppermute | solution.py:30
  246.5 0.7 copy-start.4
  248.7 0.6 copy-start
  248.7 0.6 copy-start.3
Sparse Core Ops, SparseCore 0:
  233.4 4.7 reduce-scatter.1
